TPU v7x, 32 devices: a whole 2x2x4 slice. The times are simulated.
32 devices in a mesh: dp: 4 (over y, core), mp: 8 (over z, x).
Axes of the slice: x: 2, y: 2, z: 4, core: 2. Of those that a mesh axis runs over, the one named last changes fastest.
Arguments:
- emb_grad: float32 [65536, 7168], P('dp', 'mp'), may hold values from -600 to 600
- mtp_grad: float32 [14336, 7168], P('dp', 'mp'), may hold values from -600 to 600
- emb_groups: int32 [64], replicated, may hold values from 0 to 31
- mtp_groups: int32 [32], replicated, may hold values from 0 to 31
- max_rms: float32 [1], replicated, may hold values from 0.5 to 2
Outputs:
- emb_clipped: bfloat16 [65536, 7168], P(('dp', 'mp'))
- mtp_clipped: bfloat16 [14336, 7168], P('dp', 'mp')
- group_rms: float32 [32], replicated
All inputs are finite; a program needn't handle non-finite values.
Results may differ from a plain program's by a relative error of at most 0.005.
Values may be sent and summed in bfloat16 or wider, within the bound.
A program may use at most 192 MiB of HBM per device.

v0:
```python
import jax
import jax.numpy as jnp
from jax import lax
from jax.sharding import PartitionSpec as P

D = 7168
V = 65536
CAT = 14336
EMB_BLK = 1024
MTP_BLK = 448
GROUPS = 32


def block_squares(gradient, block_rows):
    blocks = gradient.reshape(gradient.shape[0] // block_rows, block_rows, gradient.shape[1])
    return jnp.sum(jnp.square(blocks), axis=(1, 2))


def membership(labels):
    return (labels[:, None] == jnp.arange(GROUPS, dtype=jnp.int32)[None, :]).astype(jnp.float32)


def on_device(emb_grad, mtp_grad, emb_groups, mtp_groups, max_rms):
    shard = lax.axis_index("dp")
    embed_count = emb_grad.shape[0] // EMB_BLK
    head_count = mtp_grad.shape[0] // MTP_BLK
    embed_labels = lax.dynamic_slice_in_dim(emb_groups, shard * embed_count, embed_count)
    head_labels = lax.dynamic_slice_in_dim(mtp_groups, shard * head_count, head_count)
    emb_low = lax.optimization_barrier(emb_grad.astype(jnp.bfloat16))
    arrived = lax.all_to_all(emb_low, "mp", split_axis=0, concat_axis=1, tiled=True)
    partial_value = jnp.sum(
        block_squares(emb_grad, EMB_BLK)[:, None] * membership(embed_labels), axis=0
    )
    partial_value = partial_value + jnp.sum(
        block_squares(mtp_grad, MTP_BLK)[:, None] * membership(head_labels), axis=0
    )
    group_square = lax.psum(partial_value, ("dp", "mp"))
    group_size = jnp.sum(membership(emb_groups), axis=0) * jnp.float32(EMB_BLK * D) + jnp.sum(
        membership(mtp_groups), axis=0
    ) * jnp.float32(MTP_BLK * D)
    group_rms = jnp.sqrt(group_square / jnp.maximum(group_size, 1.0))
    global_norm = jnp.sqrt(jnp.sum(group_square))
    ceiling = max_rms[0] * jnp.sqrt(jnp.float32((V + CAT) * D))
    factor = ceiling / (global_norm + 1e-06)
    head_output = (mtp_grad * factor).astype(jnp.bfloat16)
    embed_output = (lax.optimization_barrier(arrived).astype(jnp.float32) * factor).astype(
        jnp.bfloat16
    )
    return (embed_output, head_output, group_rms)


def solution(mesh):
    placed = (P("dp", "mp"), P("dp", "mp"), P(), P(), P())
    return jax.shard_map(
        on_device,
        mesh=mesh,
        in_specs=placed,
        out_specs=(P(("dp", "mp"), None), P("dp", "mp"), P()),
        check_vma=False,
    )
```

profile of v0, /device:TPU:0, one launch (start us, length us, event | category | flops | bytes accessed | tf_op | source)
XLA Modules:
  0.0 817.1 jit_solution(17026694794706699184)
XLA Ops:
  0.6 46.9 %multiply_reduce_fusion = (f32[16384]{0:T(1024)S(1)}, bf16[16384,896]{1,0:T(8,128)(2,1)}) fusion(f32[16384,896]{1,0:T(8,128)} %param.5), kind=kLoop, calls=%fused_computation.1 | loop fusion | flops 44023808 | bytes 88145920 | tf_op jit(solution)/shard_map/reduce_sum | solution.py:16
  47.5 0.0 copy-start
  47.5 0.0 copy-start.1
  47.5 7.4 all-to-all-start
  54.9 5.6 multiply_reduce_fusion.1
  60.5 0.1 reduce_sum.82
  60.6 0.1 reduce_sum.83
  60.7 0.1 reduce_sum.79
  60.8 0.0 copy-done
  60.8 0.1 dynamic_slice.6
  60.9 0.0 copy-done.1
  60.9 0.1 dynamic_slice.7
  61.0 0.1 select_reduce_fusion.1
  61.1 0.1 select_reduce_fusion
  61.2 647.7 %psum.7 = f32[32]{0:T(128)S(1)} all-reduce(f32[32]{0:T(128)S(1)} %add.19), channel_id=1, replica_groups=mesh['dp'=4,'mp'=8] {'dp','mp'}, use_global_device_ids=true, to_apply=%region_6.0 | all-reduce | flops 32 | bytes 256 | tf_op jit(solution)/shard_map/psum | solution.py:37
  709.5 0.1 convert_reduce_fusion.1
  709.6 0.1 convert_reduce_fusion
  709.7 1.1 fusion
  711.6 8.4 %multiply_convert_fusion.1 = bf16[3584,896]{1,0:T(8,128)(2,1)} fusion(f32[3584,896]{1,0:T(8,128)} %param.6, f32[]{:T(128)S(6)} %div.6), kind=kLoop, calls=%fused_computation.2 | loop fusion | flops 6422528 | bytes 19267588 | tf_op jit(solution)/shard_map/convert_element_type | solution.py:45
  720.0 0.0 all-to-all-done
  720.0 40.7 %copy.11 = bf16[8,2048,896]{1,2,0:T(8,128)(2,1)} copy(bf16[8,2048,896]{2,1,0:T(8,128)(2,1)} %all-to-all-done) | data formatting | bytes 58720256 | tf_op jit(solution)/shard_map/all_to_all | solution.py:30
  760.7 20.3 %multiply_convert_fusion = bf16[2048,7168]{0,1:T(8,128)(2,1)} fusion(bf16[2048,7168]{0,1:T(8,128)(2,1)} %bitcast.5, f32[]{:T(128)S(6)} %div.6), kind=kLoop, calls=%fused_computation | loop fusion | flops 44040192 | bytes 58720260 | tf_op jit(solution)/shard_map/convert_element_type | solution.py:46
  780.9 36.2 %copy.12 = bf16[2048,7168]{1,0:T(8,128)(2,1)} copy(bf16[2048,7168]{0,1:T(8,128)(2,1)} %multiply_convert_fusion) | data formatting | bytes 58720256
  (2 shorter events, 0.0 us)
Async XLA Ops:
  47.5 13.3 %copy-start = (s32[64]{0:T(128)S(1)}, s32[64]{0:T(128)}, u32[]{:S(2)}) copy-start(s32[64]{0:T(128)} %param.7) | copy-start | bytes 772
  47.5 13.4 %copy-start.1 = (s32[32]{0:T(128)S(1)}, s32[32]{0:T(128)}, u32[]{:S(2)}) copy-start(s32[32]{0:T(128)} %param.8) | copy-start | bytes 388
  47.5 672.5 %all-to-all-start = ((bf16[8,2048,896]{2,1,0:T(8,128)(2,1)}), bf16[8,2048,896]{2,1,0:T(8,128)(2,1)}, u32[]{:S(2)}, u32[]{:S(2)}) async-start(bf16[8,2048,896]{2,1,0:T(8,128)(2,1)} %bitcast.6), calls=%async_computation | async-start | bytes 58720256 | tf_op jit(solution)/shard_map/all_to_all | solution.py:30
where the time goes:
time: 819 us; the launch traced here: 817 us
  blocking collectives  648 us (79%)
  other arithmetic  82.8 us (10%)
  local copies, waits for them, and re-layouts  77.2 us (9%)
    psum x1, blocking collectives, on_device(): group_square = lax.psum(partial_value, ('dp', 'mp'))  648 us
    reduce_sum x4, other arithmetic, block_squares(): return jnp.sum(jnp.square(blocks), axis=(1, 2))  52.7 us
    all_to_all x1, local copies, waits for them, and re-layouts, on_device(): lax.all_to_all(emb_low, 'mp', split_axis=0, concat_axis=1, tiled=True)  40.7 us
    unnamed x5, local copies, waits for them, and re-layouts  36.2 us
    convert_element_type x1, other arithmetic, on_device(): (lax.optimization_barrier(arrived).astype(jnp.float32) * factor).astype(j...  20.3 us
  transfers between devices with their start and end apart: 1, of which 0 were waited for; matrix products, arithmetic and copies ran while one was open for 2% of the time, Pallas kernels for 0%

commit v1 on v0

v1 whole, which is shorter than its diff:
```python
import functools

import jax
import jax.numpy as jnp
from jax import lax
from jax.experimental import pallas as pl
from jax.experimental.pallas import tpu as pltpu
from jax.sharding import PartitionSpec as P

EMB_BLK = 1024
MTP_BLK = 448
GROUPS = 32
STRIP = 64


def squares_kernel(x_ref, out_ref):
    height, width = x_ref.shape

    def step(i, total):
        x = x_ref[pl.ds(pl.multiple_of(i * STRIP, STRIP), STRIP), :]
        return total + jnp.sum((x * x).reshape(STRIP // 8, 8, width), axis=0)

    out_ref[0] = lax.fori_loop(0, height // STRIP, step, jnp.zeros((8, width), jnp.float32))


def block_squares(gradient, block_rows):
    rows, width = gradient.shape
    count = rows // block_rows
    sums = pl.pallas_call(
        squares_kernel,
        grid=(count,),
        in_specs=[pl.BlockSpec((block_rows, width), lambda i: (i, 0))],
        out_specs=pl.BlockSpec((1, 8, width), lambda i: (i, 0, 0)),
        out_shape=jax.ShapeDtypeStruct((count, 8, width), jnp.float32),
        cost_estimate=pl.CostEstimate(
            flops=2 * rows * width, bytes_accessed=4 * rows * width, transcendentals=0
        ),
    )(gradient)
    return jnp.sum(sums, axis=(1, 2))


def round_kernel(x_ref, out_ref):
    out_ref[...] = x_ref[...].astype(jnp.bfloat16)


def rounded_rows(by_owner, first, last, tile):
    pieces, _, width = by_owner.shape
    count = last - first
    start = first // tile
    size = pieces * count * width
    return pl.pallas_call(
        round_kernel,
        grid=(count // tile,),
        in_specs=[pl.BlockSpec((pieces, tile, width), lambda i: (0, start + i, 0))],
        out_specs=pl.BlockSpec((pieces, tile, width), lambda i: (0, i, 0)),
        out_shape=jax.ShapeDtypeStruct((pieces, count, width), jnp.bfloat16),
        cost_estimate=pl.CostEstimate(flops=size, bytes_accessed=6 * size, transcendentals=0),
    )(by_owner)


def scale_kernel(factor_ref, x_ref, *refs):
    out_ref = refs[-1]
    pieces, _, width = x_ref.shape
    factor = factor_ref[0]
    for j in range(pieces):
        out_ref[:, j * width : (j + 1) * width] = (
            x_ref[j].astype(jnp.float32) * factor
        ).astype(jnp.bfloat16)


def scale_rows(factor, arrived, out, first, rows, tile):
    pieces, count, width = arrived.shape
    start = first // tile
    in_specs = [
        pl.BlockSpec(memory_space=pltpu.SMEM),
        pl.BlockSpec((pieces, tile, width), lambda i: (0, i, 0)),
    ]
    operands = [factor.reshape(1), arrived]
    aliases = {}
    if out is not None:
        in_specs.append(pl.BlockSpec(memory_space=pl.ANY))
        operands.append(out)
        aliases = {2: 0}
    return pl.pallas_call(
        scale_kernel,
        grid=(count // tile,),
        in_specs=in_specs,
        out_specs=pl.BlockSpec((tile, pieces * width), lambda i: (start + i, 0)),
        out_shape=jax.ShapeDtypeStruct((rows, pieces * width), jnp.bfloat16),
        input_output_aliases=aliases,
        cost_estimate=pl.CostEstimate(
            flops=arrived.size, bytes_accessed=4 * arrived.size, transcendentals=0
        ),
    )(*operands)


def membership(labels):
    return (labels[:, None] == jnp.arange(GROUPS, dtype=jnp.int32)[None, :]).astype(jnp.float32)


def on_device(shards, pieces, emb_grad, mtp_grad, emb_groups, mtp_groups, max_rms):
    shard = lax.axis_index("dp")
    width = emb_grad.shape[1]
    model_width = width * pieces
    total_rows = (emb_grad.shape[0] + mtp_grad.shape[0]) * shards
    rows = emb_grad.shape[0] // pieces
    tile = rows // 32
    cuts = [0, rows // 8, rows - rows // 16, rows]

    def rounded(gradient, k):
        by_owner = gradient.reshape(pieces, rows, width)
        return rounded_rows(by_owner, cuts[k], cuts[k + 1], tile)

    def exchange(low):
        return lax.all_to_all(low, "mp", split_axis=0, concat_axis=0, tiled=True)

    low = rounded(emb_grad, 0)
    arrived = [exchange(low)]

    embed_count = emb_grad.shape[0] // EMB_BLK
    head_count = mtp_grad.shape[0] // MTP_BLK
    embed_labels = lax.dynamic_slice_in_dim(emb_groups, shard * embed_count, embed_count)
    head_labels = lax.dynamic_slice_in_dim(mtp_groups, shard * head_count, head_count)
    emb_later, mtp_later, low = lax.optimization_barrier((emb_grad, mtp_grad, low))
    partial_value = jnp.sum(
        block_squares(emb_later, EMB_BLK)[:, None] * membership(embed_labels), axis=0
    )
    partial_value = partial_value + jnp.sum(
        block_squares(mtp_later, MTP_BLK)[:, None] * membership(head_labels), axis=0
    )
    later = [rounded(emb_later, k) for k in range(1, len(cuts) - 1)]
    partial_value, later = lax.optimization_barrier((partial_value, later))
    group_square = lax.psum(partial_value, ("dp", "mp"))
    group_square, later = lax.optimization_barrier((group_square, later))
    arrived += [exchange(low) for low in later]

    group_size = jnp.sum(membership(emb_groups), axis=0) * jnp.float32(
        EMB_BLK * model_width
    ) + jnp.sum(membership(mtp_groups), axis=0) * jnp.float32(MTP_BLK * model_width)
    group_rms = jnp.sqrt(group_square / jnp.maximum(group_size, 1.0))
    global_norm = jnp.sqrt(jnp.sum(group_square))
    ceiling = max_rms[0] * jnp.sqrt(jnp.float32(total_rows * model_width))
    factor = ceiling / (global_norm + 1e-06)
    head_output = (mtp_grad * factor).astype(jnp.bfloat16)
    out = None
    for k, block in enumerate(arrived):
        out = scale_rows(factor, block, out, cuts[k], rows, tile)
    return (out, head_output, group_rms)


def solution(mesh):
    placed = (P("dp", "mp"), P("dp", "mp"), P(), P(), P())
    return jax.shard_map(
        functools.partial(on_device, mesh.shape["dp"], mesh.shape["mp"]),
        mesh=mesh,
        in_specs=placed,
        out_specs=(P(("dp", "mp"), None), P("dp", "mp"), P()),
        check_vma=False,
    )
```

time: 819 us -> 698 us (0.85)
  Pallas kernels: 0 us -> 105 us
  blocking collectives: 648 us -> 565 us
  local copies, waits for them, and re-layouts: 77.2 us -> 1.41 us
  other arithmetic: 82.8 us -> 12.2 us
    psum x1, blocking collectives: 648 us -> 40.7 us  [on_device(): group_square = lax.psum(partial_value, ('dp', 'mp'))]
    all_to_all x0 -> x1, blocking collectives: none -> 525 us  [exchange(): return lax.all_to_all(low, 'mp', split_axis=0, concat_axis=0, tiled=True)]
    pallas_call x0 -> x8, Pallas kernels: none -> 105 us  [the longest x3 40 us: rounded_rows(): pl.pallas_call(round_kernel, grid=(count // tile,), in_specs=[pl.BlockSpe...]
    reduce_sum x8 -> x6, other arithmetic: 53 us -> 2.71 us  [the longest x2 2.34 us: block_squares(): return jnp.sum(sums, axis=(1, 2))]
    all_to_all x1 -> x0, local copies, waits for them, and re-layouts: 40.7 us -> none  [on_device(): lax.all_to_all(emb_low, 'mp', split_axis=0, concat_axis=1, tiled=True)]
    unnamed x5 -> x6, local copies, waits for them, and re-layouts: 36.2 us -> 1.26 us
    convert_element_type x1 -> x0, other arithmetic: 20.3 us -> none  [on_device(): (lax.optimization_barrier(arrived).astype(jnp.float32) * factor).astype(j...]
  transfers between devices with their start and end apart: 1 -> 2, of which waited for: 0 -> 0; matrix products, arithmetic and copies ran while one was open for 2% -> 2% of each run, Pallas kernels for 0% -> 14%
where the time goes in v1:
time: 698 us; the launch traced here: 697 us
  blocking collectives  565 us (81%)
  Pallas kernels  105 us (15%)
  other arithmetic  12.2 us (2%)
  starting transfers between devices  10.9 us (2%)
    all_to_all x1, blocking collectives, exchange(): return lax.all_to_all(low, 'mp', split_axis=0, concat_axis=0, tiled=True)  525 us
    psum x1, blocking collectives, on_device(): group_square = lax.psum(partial_value, ('dp', 'mp'))  40.7 us
    pallas_call x3, Pallas kernels, rounded_rows(): pl.pallas_call(round_kernel, grid=(count // tile,), in_specs=[pl.BlockSpe...  40 us
    pallas_call x3, Pallas kernels, scale_rows(): pl.pallas_call(scale_kernel, grid=(count // tile,), in_specs=in_specs, ou...  34.3 us
    pallas_call x2, Pallas kernels, block_squares(): pl.pallas_call(squares_kernel, grid=(count,), in_specs=[pl.BlockSpec((blo...  30.4 us
  transfers between devices with their start and end apart: 2, of which 0 were waited for; matrix products, arithmetic and copies ran while one was open for 2% of the time, Pallas kernels for 14%

profile of v1, /device:TPU:0, one launch (start us, length us, event | category | flops | bytes accessed | tf_op | source)
XLA Modules:
  0.0 696.5 jit_solution(9527447064666802837)
XLA Ops:
  0.6 5.4 shard_map.76
  6.0 7.3 %all-to-all-start.2 = ((bf16[8,256,896]{2,1,0:T(8,128)(2,1)}), bf16[8,256,896]{2,1,0:T(8,128)(2,1)}, u32[]{:S(2)}, u32[]{:S(2)}) async-start(bf16[8,256,896]{2,1,0:T(8,128)(2,1)} %shard_map.76), calls=%async_computation.2 | async-start | bytes 7340032 | tf_op jit(solution)/shard_map/all_to_all | solution.py:115
  13.3 22.6 %shard_map.77 = f32[16,8,896]{2,1,0:T(8,128)} custom-call(f32[16384,896]{1,0:T(8,128)} %x_ref), custom_call_target="tpu_custom_call" | custom-call | flops 29360128 | bytes 58720256 | tf_op jit(solution)/shard_map/pallas_call | solution.py:29
  35.9 0.0 copy-start.1
  35.9 0.0 copy-start.2
  35.9 1.3 reduce_sum.63
  37.1 7.9 %shard_map.78 = f32[8,8,896]{2,1,0:T(8,128)} custom-call(f32[3584,896]{1,0:T(8,128)} %x_ref.1), custom_call_target="tpu_custom_call" | custom-call | flops 6422528 | bytes 12845056 | tf_op jit(solution)/shard_map/pallas_call | solution.py:29
  45.0 1.1 reduce_sum.65
  46.1 0.0 copy-done.1
  46.1 0.1 dynamic_slice.6
  46.2 0.0 copy-done.2
  46.2 0.1 dynamic_slice.7
  46.2 0.1 select_reduce_fusion
  46.3 0.1 select_reduce_fusion.1
  46.4 3.1 shard_map.80
  49.5 31.5 %shard_map.79 = bf16[8,1664,896]{2,1,0:T(8,128)(2,1)} custom-call(f32[8,2048,896]{2,1,0:T(8,128)} %bitcast.6), custom_call_target="tpu_custom_call" | custom-call | flops 11927552 | bytes 71565312 | tf_op jit(solution)/shard_map/pallas_call | solution.py:51
  81.0 40.7 %psum.7 = f32[32]{0:T(128)S(1)} all-reduce(f32[32]{0:T(128)S(1)} %add.19), channel_id=1, replica_groups=mesh['dp'=4,'mp'=8] {'dp','mp'}, use_global_device_ids=true, to_apply=%region_4.0 | all-reduce | flops 32 | bytes 256 | tf_op jit(solution)/shard_map/psum | solution.py:133
  121.7 0.0 all-to-all-done.2.x_ref
  121.7 524.6 %all_to_all.15.x_ref = bf16[8,1664,896]{2,1,0:T(8,128)(2,1)} all-to-all(bf16[8,1664,896]{2,1,0:T(8,128)(2,1)} %shard_map.79), channel_id=1, replica_groups=mesh['dp'=4,'mp'=8] {'mp'}, dimensions={0} | all-to-all | bytes 47710208 | tf_op jit(solution)/shard_map/all_to_all | solution.py:115
  646.3 3.6 all-to-all-start
  650.5 0.1 convert_reduce_fusion.1
  650.7 0.1 convert_reduce_fusion
  650.7 1.1 fusion
  652.6 8.4 %multiply_convert_fusion = bf16[3584,896]{1,0:T(8,128)(2,1)} fusion(f32[3584,896]{1,0:T(8,128)} %x_ref.1, f32[]{:T(128)} %div.6), kind=kLoop, calls=%fused_computation | loop fusion | flops 6422528 | bytes 19267588 | tf_op jit(solution)/shard_map/convert_element_type | solution.py:144
  661.0 4.6 shard_map.81.refs_0_
  665.6 27.1 %shard_map.82.refs_0_ = bf16[2048,7168]{1,0:T(8,128)(2,1)} custom-call(f32[1]{0:T(128)} %bitcast.3.factor_ref, bf16[8,1664,896]{2,1,0:T(8,128)(2,1)} %all_to_all.15.x_ref, bf16[2048,7168]{1,0:T(8,128)(2,1)} %shard_map.81.refs_0_), custom_call_target="tpu_custom_call", output_to_operand_aliasing={{}: (2, {})} | custom-call | flops 11927552 | bytes 47710208 | tf_op jit(solution)/shard_map/pallas_call | solution.py:84
  692.7 0.0 all-to-all-done.x_ref
  692.7 0.0 copy-start
  692.7 1.3 copy-done
  694.0 2.6 shard_map.83
  (1 shorter events, 0.0 us)
Async XLA Ops:
  6.0 115.6 %all-to-all-start.2 = ((bf16[8,256,896]{2,1,0:T(8,128)(2,1)}), bf16[8,256,896]{2,1,0:T(8,128)(2,1)}, u32[]{:S(2)}, u32[]{:S(2)}) async-start(bf16[8,256,896]{2,1,0:T(8,128)(2,1)} %shard_map.76), calls=%async_computation.2 | async-start | bytes 7340032 | tf_op jit(solution)/shard_map/all_to_all | solution.py:115
  35.9 10.2 %copy-start.1 = (s32[64]{0:T(128)S(1)}, s32[64]{0:T(128)}, u32[]{:S(2)}) copy-start(s32[64]{0:T(128)} %param.7) | copy-start | bytes 772
  35.9 10.3 %copy-start.2 = (s32[32]{0:T(128)S(1)}, s32[32]{0:T(128)}, u32[]{:S(2)}) copy-start(s32[32]{0:T(128)} %param.8) | copy-start | bytes 388
  646.3 46.4 %all-to-all-start = ((bf16[8,128,896]{2,1,0:T(8,128)(2,1)}), bf16[8,128,896]{2,1,0:T(8,128)(2,1)S(1)}, u32[]{:S(2)}, u32[]{:S(2)}) async-start(bf16[8,128,896]{2,1,0:T(8,128)(2,1)} %shard_map.80), calls=%async_computation | async-start | bytes 3670016 | tf_op jit(solution)/shard_map/all_to_all | solution.py:115
  692.7 1.3 copy-start
